TPU v7x, 32 devices: a whole 2x2x4 slice. The times are simulated.
32 devices in a mesh: row: 4 (over x, core), col: 4 (over z), layer: 2 (over y).
Axes of the slice: x: 2, y: 2, z: 4, core: 2. Of those that a mesh axis runs over, the one named last changes fastest.
Arguments:
- attn_values: bfloat16 [2048, 8192], P('row', ('layer', 'col')), may hold values from -6 to 6
- out_weight: bfloat16 [8192, 8192], P(('layer', 'row'), 'col'), may hold values from -0.09375 to 0.09375
Outputs:
- projected: bfloat16 [2048, 8192], P('row', ('col', 'layer'))
All inputs are finite; a program needn't handle non-finite values.
Results may differ from a plain program's by a relative error of at most 0.001.
Values may be sent and summed in bfloat16 or wider, within the bound.
A program may use at most 128 MiB of HBM per device.

v0:
```python
import jax
import jax.numpy as jnp
from jax import lax
from jax.sharding import PartitionSpec as P


def partner(x, axis, stride):
    return lax.ppermute(x, axis, [(i, i ^ 1 << stride) for i in range(lax.axis_size(axis))])


def shards(attn_values, out_weight):
    own_half = lax.all_gather(attn_values, "col", axis=1, tiled=True)
    other_part = partner(own_half, "layer", 0)
    first_layer = lax.axis_index("layer") == 0
    lower_half = jnp.where(first_layer, own_half, other_part)
    upper_half = jnp.where(first_layer, other_part, own_half)
    column_pair = lax.all_to_all(out_weight, "layer", split_axis=1, concat_axis=0, tiled=True)
    gathered = lax.all_gather(column_pair, "row", axis=0, tiled=True)
    row_count = lax.axis_size("row")
    depth_rows = out_weight.shape[0]
    stacked = gathered.reshape(row_count, 2, depth_rows, gathered.shape[1])
    weight_lower = stacked[:, 0].reshape(row_count * depth_rows, gathered.shape[1])
    weight_upper = stacked[:, 1].reshape(row_count * depth_rows, gathered.shape[1])
    summed = jnp.dot(lower_half, weight_lower, preferred_element_type=jnp.float32)
    summed = summed + jnp.dot(upper_half, weight_upper, preferred_element_type=jnp.float32)
    projected = summed.astype(jnp.bfloat16)
    return projected


def solution(mesh):
    in_specs = (P("row", ("layer", "col")), P(("layer", "row"), "col"))
    out_specs = P("row", ("col", "layer"))
    return jax.shard_map(shards, mesh=mesh, in_specs=in_specs, out_specs=out_specs, check_vma=False)
```

profile of v0, /device:TPU:0, one launch (start us, length us, event | category | flops | bytes accessed | tf_op | source)
XLA Modules:
  0.0 224.6 jit_solution(15008742448602999398)
XLA Ops:
  6.5 0.0 all-gather.3.cloned.1.call-start
  6.5 0.7 all-gather.3.cloned.1.call-update
  7.3 0.0 all-gather.5.cloned.1.call-start
  7.3 6.5 %copy.3 = bf16[1024,2048]{0,1:T(8,128)(2,1)} copy(bf16[1024,2048]{1,0:T(8,128)(2,1)} %param.3) | data formatting | bytes 8388608 | tf_op args[1]
  13.8 56.3 %all_to_all.19 = bf16[1024,2,1024]{0,2,1:T(8,128)(2,1)} all-to-all(bf16[1024,2,1024]{0,2,1:T(8,128)(2,1)} %bitcast.11), channel_id=1, replica_groups=mesh['row'=4,'col'=4,'layer'=2] {'layer'}, dimensions={1} | all-to-all | bytes 8388608 | tf_op jit(solution)/shard_map/all_to_all | solution.py:17
  70.1 6.3 %copy.4 = bf16[2,1024,1024]{2,1,0:T(8,128)(2,1)} copy(bf16[2,1024,1024]{1,2,0:T(8,128)(2,1)} %bitcast.10) | data formatting | bytes 8388608 | tf_op jit(solution)/shard_map/all_to_all | solution.py:17
  76.3 0.0 all-gather.5.cloned.1.call-update
  76.4 16.0 %all-gather.3.cloned.1.call-done = bf16[512,4096]{1,0:T(8,128)(2,1)} async-done(((bf16[512,1024]{1,0:T(8,128)(2,1)}), bf16[512,4096]{1,0:T(8,128)(2,1)}) %all-gather.3.cloned.1.call-update) | async-done | bytes 4194320 | tf_op jit(solution)/shard_map/all_gather | solution.py:12
  92.4 1.5 collective-permute-start
  93.9 104.5 %all-gather.5.cloned.1.call-done = bf16[8192,1024]{1,0:T(8,128)(2,1)} async-done(((bf16[2048,1024]{1,0:T(8,128)(2,1)}), bf16[8192,1024]{1,0:T(8,128)(2,1)}) %all-gather.5.cloned.1.call-update) | async-done | bytes 16777232 | tf_op jit(solution)/shard_map/all_gather | solution.py:18
  198.4 0.0 copy-start
  198.4 7.0 %fusion.8 = (bf16[4,1,1024,1024]{3,2,1,0:T(8,128)(2,1)S(1)}, bf16[4,1,1024,1024]{3,2,1,0:T(8,128)(2,1)S(1)}) fusion(bf16[4,2,1024,1024]{3,2,1,0:T(8,128)(2,1)} %bitcast.8), kind=kLoop, calls=%fused_computation.7 | loop fusion | bytes 33554432 | tf_op jit(solution)/shard_map/slice | solution.py:22
  205.4 0.0 collective-permute-done
  205.4 0.0 copy-done
  205.4 6.8 %fusion = f32[512,1024]{1,0:T(8,128)S(1)} fusion(bf16[4096,1024]{1,0:T(8,128)(2,1)S(1)} %bitcast.13, bf16[512,4096]{1,0:T(8,128)(2,1)} %collective-permute-done, bf16[512,4096]{1,0:T(8,128)(2,1)S(1)} %copy-done, pred[]{:T(512)S(6)} %eq.3), kind=kOutput, calls=%fused_computation | convolution fusion | flops 4297064448 | bytes 18874368 | tf_op jit(solution)/shard_map/dot_general | solution.py:25
  212.2 5.6 %add_convert_fusion = bf16[512,1024]{1,0:T(8,128)(2,1)} fusion(f32[512,1024]{1,0:T(8,128)S(1)} %fusion, bf16[4096,1024]{1,0:T(8,128)(2,1)S(1)} %bitcast.12, bf16[512,4096]{1,0:T(8,128)(2,1)S(1)} %copy-done, bf16[512,4096]{1,0:T(8,128)(2,1)} %collective-permute-done, pred[]{:T(512)S(6)} %eq.3), kind=kOutput, calls=%fused_computation.6 | convolution fusion | flops 4298113024 | bytes 19922944 | tf_op jit(solution)/shard_map/dot_general | solution.py:24
Async XLA Ops:
  6.5 85.9 %all-gather.3.cloned.1.call-start = ((), (), s32[]{:S(2)}) async-start(), calls=%async_computation.1 | async-start | bytes 5242880 | tf_op jit(solution)/shard_map/all_gather | solution.py:12
  7.3 191.1 %all-gather.5.cloned.1.call-start = ((), (), s32[]{:S(2)}) async-start(), calls=%async_computation.2 | async-start | bytes 20971520 | tf_op jit(solution)/shard_map/all_gather | solution.py:18
  92.4 113.0 %collective-permute-start = (bf16[512,4096]{1,0:T(8,128)(2,1)}, bf16[512,4096]{1,0:T(8,128)(2,1)}, u32[]{:S(2)}, u32[]{:S(2)}) collective-permute-start(bf16[512,4096]{1,0:T(8,128)(2,1)} %all-gather.3.cloned.1.call-done), channel_id=1, source_target_pairs={{0,1},{1,0},{2,3},{3,2},{4,5},{5,4},{6,7},{7,6},{8,9},{9,8},{10,11... | collective-permute-start | bytes 12582920 | tf_op jit(solution)/shard_map/ppermute | solution.py:8
  198.4 7.1 %copy-start = (bf16[512,4096]{1,0:T(8,128)(2,1)S(1)}, bf16[512,4096]{1,0:T(8,128)(2,1)}, u32[]{:S(2)}) copy-start(bf16[512,4096]{1,0:T(8,128)(2,1)} %all-gather.3.cloned.1.call-done) | copy-start | bytes 12582916
Sparse Core Ops, SparseCore 0:
  8.9 83.4 all-gather.2
  93.9 104.3 all-gather.4
where the time goes:
time: 225 us
  waiting for transfers between devices  121 us (54%)
  blocking collectives  56.3 us (25%)
  local copies, waits for them, and re-layouts  19.8 us (9%)
  between operations  13.4 us (6%)
  matrix products  12.4 us (6%)
    all_gather x1, waiting for transfers between devices, shards(): gathered = lax.all_gather(column_pair, 'row', axis=0, tiled=True)  104 us
    all_to_all x1, blocking collectives, shards(): lax.all_to_all(out_weight, 'layer', split_axis=1, concat_axis=0, tiled=True)  56.3 us
    all_gather x1, waiting for transfers between devices, shards(): own_half = lax.all_gather(attn_values, 'col', axis=1, tiled=True)  16 us
    slice x1, local copies, waits for them, and re-layouts, shards(): stacked[:, 0].reshape(row_count * depth_rows, gathered.shape[1])  6.99 us
    dot_general x1, matrix products, shards(): jnp.dot(upper_half, weight_upper, preferred_element_type=jnp.float32)  6.79 us
    unnamed x3, local copies, waits for them, and re-layouts  6.5 us
    all_to_all x1, local copies, waits for them, and re-layouts, shards(): lax.all_to_all(out_weight, 'layer', split_axis=1, concat_axis=0, tiled=True)  6.26 us
    dot_general x1, matrix products, shards(): jnp.dot(lower_half, weight_lower, preferred_element_type=jnp.float32)  5.57 us
  transfers between devices with their start and end apart: 3, of which 2 were waited for; matrix products, arithmetic and copies ran while one was open for 9% of the time, Pallas kernels for 0%

commit v1 on v0

--- a/solution.py
+++ b/solution.py
@@ -14,7 +14,12 @@
     first_layer = lax.axis_index("layer") == 0
     lower_half = jnp.where(first_layer, own_half, other_part)
     upper_half = jnp.where(first_layer, other_part, own_half)
-    column_pair = lax.all_to_all(out_weight, "layer", split_axis=1, concat_axis=0, tiled=True)
+    column_pair = jnp.concatenate(
+        lax.all_to_all(
+            jnp.stack(jnp.split(out_weight, lax.axis_size("layer"), axis=1)), "layer", 0, 0
+        ),
+        axis=0,
+    )
     gathered = lax.all_gather(column_pair, "row", axis=0, tiled=True)
     row_count = lax.axis_size("row")
     depth_rows = out_weight.shape[0]

time: 225 us -> 225 us (level)
  waiting for transfers between devices: 121 us -> 135 us
  local copies, waits for them, and re-layouts: 19.8 us -> 9.7 us
  blocking collectives: 56.3 us -> 52.6 us
    all_gather x1, waiting for transfers between devices: 16 us -> 29.4 us  [shards(): own_half = lax.all_gather(attn_values, 'col', axis=1, tiled=True)]
    unnamed x3 -> x2, local copies, waits for them, and re-layouts: 6.5 us -> 0.04 us
    all_to_all x1 -> x0, local copies, waits for them, and re-layouts: 6.26 us -> none  [shards(): lax.all_to_all(out_weight, 'layer', split_axis=1, concat_axis=0, tiled=True)]
    all_to_all x1, blocking collectives: 56.3 us -> 52.6 us  [shards(): lax.all_to_all(jnp.stack(jnp.split(out_weight, lax.axis_size('layer'), ax...]
    another operation x0 -> x1, local copies, waits for them, and re-layouts: none -> 2.66 us  [shards(): jnp.stack(jnp.split(out_weight, lax.axis_size('layer'), axis=1))]
  transfers between devices with their start and end apart: 3 -> 3, of which waited for: 2 -> 2; matrix products, arithmetic and copies ran while one was open for 9% -> 4% of each run, Pallas kernels for 0% -> 0%
where the time goes in v1:
time: 225 us
  waiting for transfers between devices  135 us (60%)
  blocking collectives  52.6 us (23%)
  between operations  13.4 us (6%)
  matrix products  12.4 us (6%)
  local copies, waits for them, and re-layouts  9.7 us (4%)
    all_gather x1, waiting for transfers between devices, shards(): gathered = lax.all_gather(column_pair, 'row', axis=0, tiled=True)  104 us
    all_to_all x1, blocking collectives, shards(): lax.all_to_all(jnp.stack(jnp.split(out_weight, lax.axis_size('layer'), ax...  52.6 us
    all_gather x1, waiting for transfers between devices, shards(): own_half = lax.all_gather(attn_values, 'col', axis=1, tiled=True)  29.4 us
    slice x1, local copies, waits for them, and re-layouts, shards(): stacked[:, 0].reshape(row_count * depth_rows, gathered.shape[1])  6.99 us
    dot_general x1, matrix products, shards(): jnp.dot(upper_half, weight_upper, preferred_element_type=jnp.float32)  6.79 us
    dot_general x1, matrix products, shards(): jnp.dot(lower_half, weight_lower, preferred_element_type=jnp.float32)  5.57 us
  transfers between devices with their start and end apart: 3, of which 2 were waited for; matrix products, arithmetic and copies ran while one was open for 4% of the time, Pallas kernels for 0%

profile of v1, /device:TPU:0, one launch (start us, length us, event | category | flops | bytes accessed | tf_op | source)
XLA Modules:
  0.0 224.6 jit_solution(3076637762112578204)
XLA Ops:
  6.5 0.0 all-gather.3.cloned.1.call-start
  6.5 0.7 all-gather.3.cloned.1.call-update
  7.3 0.0 all-gather.5.cloned.1.call-start
  7.3 2.7 %slice_bitcast_fusion.1 = (bf16[1,1024,1024]{2,1,0:T(8,128)(2,1)S(1)}, bf16[1,1024,1024]{2,1,0:T(8,128)(2,1)S(1)}) fusion(bf16[1024,2048]{1,0:T(8,128)(2,1)} %param.3), kind=kLoop, calls=%fused_computation.9 | loop fusion | bytes 8388608 | tf_op jit(solution)/shard_map/stack | solution.py:19
  10.0 0.4 pad_maximum_fusion
  10.4 52.6 %all_to_all.5 = bf16[2,1024,1024]{2,1,0:T(8,128)(2,1)} all-to-all(bf16[2,1024,1024]{2,1,0:T(8,128)(2,1)S(1)} %pad_maximum_fusion), channel_id=1, replica_groups=mesh['row'=4,'col'=4,'layer'=2] {'layer'}, dimensions={0} | all-to-all | bytes 8388608 | tf_op jit(solution)/shard_map/all_to_all | solution.py:18
  63.0 0.0 all-gather.5.cloned.1.call-update
  63.0 29.4 %all-gather.3.cloned.1.call-done = bf16[512,4096]{1,0:T(8,128)(2,1)} async-done(((bf16[512,1024]{1,0:T(8,128)(2,1)}), bf16[512,4096]{1,0:T(8,128)(2,1)}) %all-gather.3.cloned.1.call-update) | async-done | bytes 4194320 | tf_op jit(solution)/shard_map/all_gather | solution.py:12
  92.4 1.5 collective-permute-start
  93.9 104.5 %all-gather.5.cloned.1.call-done = bf16[8192,1024]{1,0:T(8,128)(2,1)} async-done(((bf16[2048,1024]{1,0:T(8,128)(2,1)}), bf16[8192,1024]{1,0:T(8,128)(2,1)}) %all-gather.5.cloned.1.call-update) | async-done | bytes 16777232 | tf_op jit(solution)/shard_map/all_gather | solution.py:23
  198.4 0.0 copy-start
  198.4 7.0 %fusion.8 = (bf16[4,1,1024,1024]{3,2,1,0:T(8,128)(2,1)S(1)}, bf16[4,1,1024,1024]{3,2,1,0:T(8,128)(2,1)S(1)}) fusion(bf16[4,2,1024,1024]{3,2,1,0:T(8,128)(2,1)} %bitcast.10), kind=kLoop, calls=%fused_computation.10 | loop fusion | bytes 33554432 | tf_op jit(solution)/shard_map/slice | solution.py:27
  205.4 0.0 collective-permute-done
  205.4 0.0 copy-done
  205.4 6.8 %fusion = f32[512,1024]{1,0:T(8,128)S(1)} fusion(bf16[4096,1024]{1,0:T(8,128)(2,1)S(1)} %bitcast.13, bf16[512,4096]{1,0:T(8,128)(2,1)} %collective-permute-done, bf16[512,4096]{1,0:T(8,128)(2,1)S(1)} %copy-done, pred[]{:T(512)S(6)} %eq.3), kind=kOutput, calls=%fused_computation.1 | convolution fusion | flops 4297064448 | bytes 18874368 | tf_op jit(solution)/shard_map/dot_general | solution.py:30
  212.2 5.6 %add_convert_fusion = bf16[512,1024]{1,0:T(8,128)(2,1)} fusion(f32[512,1024]{1,0:T(8,128)S(1)} %fusion, bf16[4096,1024]{1,0:T(8,128)(2,1)S(1)} %bitcast.12, bf16[512,4096]{1,0:T(8,128)(2,1)S(1)} %copy-done, bf16[512,4096]{1,0:T(8,128)(2,1)} %collective-permute-done, pred[]{:T(512)S(6)} %eq.3), kind=kOutput, calls=%fused_computation.7 | convolution fusion | flops 4298113024 | bytes 19922944 | tf_op jit(solution)/shard_map/dot_general | solution.py:29
Async XLA Ops:
  6.5 85.9 %all-gather.3.cloned.1.call-start = ((), (), s32[]{:S(2)}) async-start(), calls=%async_computation.1 | async-start | bytes 5242880 | tf_op jit(solution)/shard_map/all_gather | solution.py:12
  7.3 191.1 %all-gather.5.cloned.1.call-start = ((), (), s32[]{:S(2)}) async-start(), calls=%async_computation.2 | async-start | bytes 20971520 | tf_op jit(solution)/shard_map/all_gather | solution.py:23
  92.4 113.0 %collective-permute-start = (bf16[512,4096]{1,0:T(8,128)(2,1)}, bf16[512,4096]{1,0:T(8,128)(2,1)}, u32[]{:S(2)}, u32[]{:S(2)}) collective-permute-start(bf16[512,4096]{1,0:T(8,128)(2,1)} %all-gather.3.cloned.1.call-done), channel_id=1, source_target_pairs={{0,1},{1,0},{2,3},{3,2},{4,5},{5,4},{6,7},{7,6},{8,9},{9,8},{10,11... | collective-permute-start | bytes 12582920 | tf_op jit(solution)/shard_map/ppermute | solution.py:8
  198.4 7.1 %copy-start = (bf16[512,4096]{1,0:T(8,128)(2,1)S(1)}, bf16[512,4096]{1,0:T(8,128)(2,1)}, u32[]{:S(2)}) copy-start(bf16[512,4096]{1,0:T(8,128)(2,1)} %all-gather.3.cloned.1.call-done) | copy-start | bytes 12582916
Sparse Core Ops, SparseCore 0:
  8.9 83.4 all-gather.2
  93.9 104.3 all-gather.4

commit v2 on v0

--- a/solution.py
+++ b/solution.py
@@ -15,7 +15,12 @@
     lower_half = jnp.where(first_layer, own_half, other_part)
     upper_half = jnp.where(first_layer, other_part, own_half)
     column_pair = lax.all_to_all(out_weight, "layer", split_axis=1, concat_axis=0, tiled=True)
-    gathered = lax.all_gather(column_pair, "row", axis=0, tiled=True)
+    ring = [column_pair]
+    for hop in range(3):
+        ring.append(lax.ppermute(ring[-1], "row", [(dev, (dev + 1) % 4) for dev in range(4)]))
+    gathered = jnp.roll(
+        jnp.concatenate(ring[::-1], axis=0), (lax.axis_index("row") + 1) * ring[0].shape[0], axis=0
+    )
     row_count = lax.axis_size("row")
     depth_rows = out_weight.shape[0]
     stacked = gathered.reshape(row_count, 2, depth_rows, gathered.shape[1])

time: 225 us -> 319 us (1.42)
  waiting for transfers between devices: 121 us -> 179 us
  local copies, waits for them, and re-layouts: 19.8 us -> 55 us
    ppermute x0 -> x3, waiting for transfers between devices: none -> 110 us  [shards(): lax.ppermute(ring[-1], 'row', [(dev, (dev + 1) % 4) for dev in range(4)])]
    all_gather x1 -> x0, waiting for transfers between devices: 104 us -> none  [shards(): gathered = lax.all_gather(column_pair, 'row', axis=0, tiled=True)]
    ppermute x1, waiting for transfers between devices: 0.01 us -> 35.3 us  [partner(): lax.ppermute(x, axis, [(i, i ^ 1 << stride) for i in range(lax.axis_size(...]
    unnamed x3 -> x12, local copies, waits for them, and re-layouts: 6.5 us -> 36.5 us
    all_gather x1, waiting for transfers between devices: 16 us -> 33.5 us  [shards(): own_half = lax.all_gather(attn_values, 'col', axis=1, tiled=True)]
    dynamic_slice x0 -> x1, local copies, waits for them, and re-layouts: none -> 8.13 us  [shards(): jnp.roll(jnp.concatenate(ring[::-1], axis=0), (lax.axis_index('row') + 1)...]
    slice x1, local copies, waits for them, and re-layouts: 6.99 us -> 1.83 us  [shards(): stacked[:, 0].reshape(row_count * depth_rows, gathered.shape[1])]
  transfers between devices with their start and end apart: 3 -> 5, of which waited for: 2 -> 5; matrix products, arithmetic and copies ran while one was open for 9% -> 13% of each run, Pallas kernels for 0% -> 0%
where the time goes in v2:
time: 319 us; the launch traced here: 317 us
  waiting for transfers between devices  179 us (56%)
  blocking collectives  56.3 us (18%)
  local copies, waits for them, and re-layouts  55 us (17%)
  between operations  13.4 us (4%)
  matrix products  12.3 us (4%)
    ppermute x3, waiting for transfers between devices, shards(): lax.ppermute(ring[-1], 'row', [(dev, (dev + 1) % 4) for dev in range(4)])  110 us
    all_to_all x1, blocking collectives, shards(): lax.all_to_all(out_weight, 'layer', split_axis=1, concat_axis=0, tiled=True)  56.3 us
    unnamed x12, local copies, waits for them, and re-layouts  36.5 us
    ppermute x1, waiting for transfers between devices, partner(): lax.ppermute(x, axis, [(i, i ^ 1 << stride) for i in range(lax.axis_size(...  35.3 us
    all_gather x1, waiting for transfers between devices, shards(): own_half = lax.all_gather(attn_values, 'col', axis=1, tiled=True)  33.5 us
    dynamic_slice x1, local copies, waits for them, and re-layouts, shards(): jnp.roll(jnp.concatenate(ring[::-1], axis=0), (lax.axis_index('row') + 1)...  8.13 us
    dot_general x1, matrix products, shards(): jnp.dot(upper_half, weight_upper, preferred_element_type=jnp.float32)  6.67 us
  transfers between devices with their start and end apart: 5, of which 5 were waited for; matrix products, arithmetic and copies ran while one was open for 13% of the time, Pallas kernels for 0%

profile of v2, /device:TPU:0, one launch (start us, length us, event | category | flops | bytes accessed | tf_op | source)
XLA Modules:
  0.0 317.1 jit_solution(906530326872129639)
XLA Ops:
  6.5 0.0 all-gather.2.cloned.1.call-start
  6.5 6.4 %copy.3 = bf16[1024,2048]{0,1:T(8,128)(2,1)} copy(bf16[1024,2048]{1,0:T(8,128)(2,1)} %param.3) | data formatting | bytes 8388608 | tf_op args[1]
  13.0 56.3 %all_to_all.19 = bf16[1024,2,1024]{0,2,1:T(8,128)(2,1)} all-to-all(bf16[1024,2,1024]{0,2,1:T(8,128)(2,1)} %bitcast.13), channel_id=1, replica_groups=mesh['row'=4,'col'=4,'layer'=2] {'layer'}, dimensions={1} | all-to-all | bytes 8388608 | tf_op jit(solution)/shard_map/all_to_all | solution.py:17
  69.3 6.2 %copy.4 = bf16[2,1024,1024]{2,1,0:T(8,128)(2,1)} copy(bf16[2,1024,1024]{1,2,0:T(8,128)(2,1)} %bitcast.12) | data formatting | bytes 8388608 | tf_op jit(solution)/shard_map/all_to_all | solution.py:17
  75.4 0.0 collective-permute-start.1
  75.4 48.2 %collective-permute-done.1 = bf16[2048,1024]{1,0:T(8,128)(2,1)} collective-permute-done((bf16[2048,1024]{1,0:T(8,128)(2,1)}, bf16[2048,1024]{1,0:T(8,128)(2,1)}, u32[]{:S(2)}, u32[]{:S(2)}) %collective-permute-start.1) | collective-permute-done | bytes 4194336 | tf_op jit(solution)/shard_map/ppermute | solution.py:20
  123.7 0.0 collective-permute-start.2
  123.7 0.0 all-gather.2.cloned.1.call-update
  123.7 48.2 %collective-permute-done.2 = bf16[2048,1024]{1,0:T(8,128)(2,1)} collective-permute-done((bf16[2048,1024]{1,0:T(8,128)(2,1)}, bf16[2048,1024]{1,0:T(8,128)(2,1)}, u32[]{:S(2)}, u32[]{:S(2)}) %collective-permute-start.2) | collective-permute-done | bytes 4194336 | tf_op jit(solution)/shard_map/ppermute | solution.py:20
  171.9 0.0 collective-permute-start.3
  171.9 33.5 %all-gather.2.cloned.1.call-done = bf16[512,4096]{1,0:T(8,128)(2,1)} async-done(((bf16[512,1024]{1,0:T(8,128)(2,1)}), bf16[512,4096]{1,0:T(8,128)(2,1)}) %all-gather.2.cloned.1.call-update) | async-done | bytes 4194320 | tf_op jit(solution)/shard_map/all_gather | solution.py:12
  205.5 1.5 collective-permute-start
  206.9 13.3 %collective-permute-done.3 = bf16[2048,1024]{1,0:T(8,128)(2,1)} collective-permute-done((bf16[2048,1024]{1,0:T(8,128)(2,1)}, bf16[2048,1024]{1,0:T(8,128)(2,1)}, u32[]{:S(2)}, u32[]{:S(2)}) %collective-permute-start.3) | collective-permute-done | bytes 4194336 | tf_op jit(solution)/shard_map/ppermute | solution.py:20
  220.2 4.6 %constant_dynamic-update-slice_fusion.7 = bf16[16384,1024]{1,0:T(8,128)(2,1)} fusion(bf16[2048,1024]{1,0:T(8,128)(2,1)} %collective-permute-done.3), kind=kLoop, calls=%fused_computation.14 | loop fusion | bytes 8388608
  224.8 0.0 copy-start
  224.8 4.8 %constant_dynamic-update-slice_fusion.6 = bf16[16384,1024]{1,0:T(8,128)(2,1)} fusion(bf16[16384,1024]{1,0:T(8,128)(2,1)} %constant_dynamic-update-slice_fusion.7, bf16[2048,1024]{1,0:T(8,128)(2,1)} %collective-permute-done.2), kind=kLoop, calls=%fused_computation.13 | loop fusion | bytes 8388608
  229.5 4.6 %constant_dynamic-update-slice_fusion.5 = bf16[16384,1024]{1,0:T(8,128)(2,1)} fusion(bf16[16384,1024]{1,0:T(8,128)(2,1)} %constant_dynamic-update-slice_fusion.6, bf16[2048,1024]{1,0:T(8,128)(2,1)} %collective-permute-done.1), kind=kLoop, calls=%fused_computation.12 | loop fusion | bytes 8388608
  234.1 0.0 copy-done
  234.1 2.4 constant_dynamic-update-slice_fusion.4
  236.5 4.6 %constant_dynamic-update-slice_fusion.3 = bf16[16384,1024]{1,0:T(8,128)(2,1)} fusion(bf16[16384,1024]{1,0:T(8,128)(2,1)} %constant_dynamic-update-slice_fusion.4, bf16[2048,1024]{1,0:T(8,128)(2,1)} %collective-permute-done.3), kind=kLoop, calls=%fused_computation.10 | loop fusion | bytes 8388608
  241.1 4.6 %constant_dynamic-update-slice_fusion.2 = bf16[16384,1024]{1,0:T(8,128)(2,1)} fusion(bf16[16384,1024]{1,0:T(8,128)(2,1)} %constant_dynamic-update-slice_fusion.3, bf16[2048,1024]{1,0:T(8,128)(2,1)} %collective-permute-done.2), kind=kLoop, calls=%fused_computation.9 | loop fusion | bytes 8388608
  245.7 4.6 %constant_dynamic-update-slice_fusion.1 = bf16[16384,1024]{1,0:T(8,128)(2,1)} fusion(bf16[16384,1024]{1,0:T(8,128)(2,1)} %constant_dynamic-update-slice_fusion.2, bf16[2048,1024]{1,0:T(8,128)(2,1)} %collective-permute-done.1), kind=kLoop, calls=%fused_computation.8 | loop fusion | bytes 8388608
  250.3 2.4 constant_dynamic-update-slice_fusion
  252.6 8.1 %constant_dynamic-slice_fusion = bf16[8192,1024]{1,0:T(8,128)(2,1)S(1)} fusion(bf16[16384,1024]{1,0:T(8,128)(2,1)} %constant_dynamic-update-slice_fusion, s32[]{:T(128)S(6)} %select_n.28), kind=kLoop, calls=%fused_computation.15 | loop fusion | bytes 33554436 | tf_op jit(solution)/shard_map/jit(_roll_dynamic)/dynamic_slice | solution.py:21
  260.8 1.8 fusion.8
  262.6 35.3 %collective-permute-done = bf16[512,4096]{1,0:T(8,128)(2,1)} collective-permute-done((bf16[512,4096]{1,0:T(8,128)(2,1)}, bf16[512,4096]{1,0:T(8,128)(2,1)}, u32[]{:S(2)}, u32[]{:S(2)}) %collective-permute-start) | collective-permute-done | bytes 4194336 | tf_op jit(solution)/shard_map/ppermute | solution.py:8
  297.9 0.0 copy-start.1
  297.9 6.7 %fusion = f32[512,1024]{1,0:T(8,128)S(1)} fusion(bf16[4096,1024]{1,0:T(8,128)(2,1)S(1)} %bitcast.15, bf16[512,4096]{1,0:T(8,128)(2,1)} %collective-permute-done, bf16[512,4096]{1,0:T(8,128)(2,1)} %all-gather.2.cloned.1.call-done, pred[]{:T(512)S(6)} %eq.6), kind=kOutput, calls=%fused_computation | convolution fusion | flops 4297064448 | bytes 18874368 | tf_op jit(solution)/shard_map/dot_general | solution.py:30
  304.6 0.0 copy-done.1
  304.6 5.7 %add_convert_fusion = bf16[512,1024]{1,0:T(8,128)(2,1)} fusion(f32[512,1024]{1,0:T(8,128)S(1)} %fusion, bf16[4096,1024]{1,0:T(8,128)(2,1)S(1)} %bitcast.14, bf16[512,4096]{1,0:T(8,128)(2,1)S(1)} %copy-done.1, bf16[512,4096]{1,0:T(8,128)(2,1)} %collective-permute-done, pred[]{:T(512)S(6)} %eq.6), kind=kOutput, calls=%fused_computation.6 | convolution fusion | flops 4298113024 | bytes 19922944 | tf_op jit(solution)/shard_map/dot_general | solution.py:29
Async XLA Ops:
  6.5 198.9 %all-gather.2.cloned.1.call-start = ((), (), s32[]{:S(2)}) async-start(), calls=%async_computation.1 | async-start | bytes 5242880 | tf_op jit(solution)/shard_map/all_gather | solution.py:12
  75.4 48.2 %collective-permute-start.1 = (bf16[2048,1024]{1,0:T(8,128)(2,1)}, bf16[2048,1024]{1,0:T(8,128)(2,1)}, u32[]{:S(2)}, u32[]{:S(2)}) collective-permute-start(bf16[2048,1024]{1,0:T(8,128)(2,1)} %bitcast.9), channel_id=1, source_target_pairs={{0,8},{8,16},{16,24},{24,0},{1,9},{9,17},{17,25},{25,1},{2,10},{10... | collective-permute-start | bytes 12582920 | tf_op jit(solution)/shard_map/ppermute | solution.py:20
  123.7 48.2 %collective-permute-start.2 = (bf16[2048,1024]{1,0:T(8,128)(2,1)}, bf16[2048,1024]{1,0:T(8,128)(2,1)}, u32[]{:S(2)}, u32[]{:S(2)}) collective-permute-start(bf16[2048,1024]{1,0:T(8,128)(2,1)} %collective-permute-done.1), channel_id=1, source_target_pairs={{0,8},{8,16},{16,24},{24,0},{1,9},{9,17},{17,25},{25,1},{2,10},{10... | collective-permute-start | bytes 12582920 | tf_op jit(solution)/shard_map/ppermute | solution.py:20
  171.9 48.2 %collective-permute-start.3 = (bf16[2048,1024]{1,0:T(8,128)(2,1)}, bf16[2048,1024]{1,0:T(8,128)(2,1)}, u32[]{:S(2)}, u32[]{:S(2)}) collective-permute-start(bf16[2048,1024]{1,0:T(8,128)(2,1)} %collective-permute-done.2), channel_id=1, source_target_pairs={{0,8},{8,16},{16,24},{24,0},{1,9},{9,17},{17,25},{25,1},{2,10},{10... | collective-permute-start | bytes 12582920 | tf_op jit(solution)/shard_map/ppermute | solution.py:20
  205.5 92.5 %collective-permute-start = (bf16[512,4096]{1,0:T(8,128)(2,1)}, bf16[512,4096]{1,0:T(8,128)(2,1)}, u32[]{:S(2)}, u32[]{:S(2)}) collective-permute-start(bf16[512,4096]{1,0:T(8,128)(2,1)} %all-gather.2.cloned.1.call-done), channel_id=1, source_target_pairs={{0,1},{1,0},{2,3},{3,2},{4,5},{5,4},{6,7},{7,6},{8,9},{9,8},{10,11... | collective-permute-start | bytes 12582920 | tf_op jit(solution)/shard_map/ppermute | solution.py:8
  224.8 9.4 %copy-start = (bf16[2,1024,1024]{2,1,0:T(8,128)(2,1)S(1)}, bf16[2,1024,1024]{2,1,0:T(8,128)(2,1)}, u32[]{:S(2)}) copy-start(bf16[2,1024,1024]{2,1,0:T(8,128)(2,1)} %copy.4) | copy-start | bytes 12582916
  297.9 6.7 %copy-start.1 = (bf16[512,4096]{1,0:T(8,128)(2,1)S(1)}, bf16[512,4096]{1,0:T(8,128)(2,1)}, u32[]{:S(2)}) copy-start(bf16[512,4096]{1,0:T(8,128)(2,1)} %all-gather.2.cloned.1.call-done) | copy-start | bytes 12582916
Sparse Core Ops, SparseCore 0:
  123.8 81.5 all-gather.1
